TPU v7x, 32 devices: a whole 2x2x4 slice. The times are simulated.
32 devices in a mesh: blk: 16 (over z, y, core), along: 2 (over x).
Axes of the slice: x: 2, y: 2, z: 4, core: 2. Of those that a mesh axis runs over, the one named last changes fastest.
Arguments:
- values: float32 [3, 16, 48, 256], P(None, 'blk', 'along'), may hold values from -6 to 6
- offsets: float32 [3, 16, 48, 256], P(None, 'blk', 'along'), may hold values from 0 to 1
- stiffness: float32 [16, 48, 256], P('blk', 'along'), may hold values from 0.5 to 2
- leaf_basis: float32 [16, 48, 64, 256], P('blk', 'along'), may hold values from -0.375 to 0.375
- transfer: float32 [16, 48, 64, 64], P('blk', 'along'), may hold values from -0.15625 to 0.15625
- slab_transfer_matrices: float32 [16, 2, 64, 64], P('blk', 'along'), may hold values from -0.5 to 0.5
- leaf_coupling_matrices: float32 [16, 30, 64, 64], P('blk'), may hold values from -0.375 to 0.375
- leaf_admissible_mask: int32 [16, 30], P('blk'), may hold values 0 or 1
- top_coupling: float32 [16, 16, 64, 64], P('blk'), may hold values from -0.75 to 0.75
- top_admissible: int32 [16, 16], P('blk'), may hold values 0 or 1
Outputs:
- product: float32 [3, 16, 48, 256], P(None, 'blk', 'along')
All inputs are finite; a program needn't handle non-finite values. No bound on the sum of `leaf_admissible_mask` or of `top_admissible` on one device may be relied on, other than what follows from the above.
Results may differ from a plain program's by a relative error of at most 0.0001.
Values sent between devices are 32-bit elements; how exact they have to be, the bound alone decides.
A program may use at most 64 MiB of HBM per device.

v0:
```python
import jax
import jax.numpy as jnp
from jax import lax
from jax.sharding import PartitionSpec as P

REACH = 6
SHARPNESS = 2.0
KERNEL_SCALE = 0.125
HIGHEST_ACCURACY = lax.Precision.HIGHEST


def with_halo(cells, sides, width, closed):
    for axis, dim in sides:
        count = lax.axis_size(axis)
        ends = count if closed else count - 1
        head = lax.slice_in_dim(cells, 0, width, axis=dim)
        tail = lax.slice_in_dim(cells, cells.shape[dim] - width, cells.shape[dim], axis=dim)
        cells = jnp.concatenate(
            [
                lax.ppermute(tail, axis, [(i, (i + 1) % count) for i in range(ends)]),
                cells,
                lax.ppermute(head, axis, [((i + 1) % count, i) for i in range(ends)]),
            ],
            axis=dim,
        )
    return cells


def passed_along(x, axis, by):
    count = lax.axis_size(axis)
    return lax.ppermute(x, axis, [(i, (i + by) % count) for i in range(count)])


def near_field(padded):
    leaves = padded.shape[2] - 2
    center = padded[:, 1:2, 1 : 1 + leaves]
    result = jnp.zeros((3, 1, leaves, padded.shape[3]), jnp.float32)
    for around in (-1, 0, 1):
        for along_step in (-1, 0, 1):
            source = padded[:, 1 + around : 2 + around, 1 + along_step : 1 + along_step + leaves]
            gap_around = around + source[0][..., None, :] - center[0][..., :, None]
            gap_along = along_step + source[1][..., None, :] - center[1][..., :, None]
            gap_radial = source[2][..., None, :] - center[2][..., :, None]
            squared = gap_around * gap_around + gap_along * gap_along + gap_radial * gap_radial
            kernel = (
                KERNEL_SCALE
                * center[3][..., :, None]
                * source[3][..., None, :]
                * jnp.exp(-SHARPNESS * squared)
            )
            result = result + jnp.einsum(
                "alij,ralj->rali", kernel, source[4:], precision=HIGHEST_ACCURACY
            )
    return result


def slot_number(around, along_step, reach):
    block = around - 2 if around > 0 else reach - 1 + (-around - 2)
    return 3 * block + along_step + 1


def add_sector(total, held, around, leaf_coupling_matrices, leaf_admissible_mask):
    leaves = total.shape[2]
    for along_step in (-1, 0, 1):
        slot = slot_number(around, along_step, REACH)
        partner = held[:, :, 1 + along_step : 1 + along_step + leaves]
        coupling = (
            leaf_coupling_matrices[:, slot]
            * leaf_admissible_mask[:, slot].astype(jnp.float32)[:, None, None]
        )
        total = total + jnp.einsum("skq,rslq->rslk", coupling, partner, precision=HIGHEST_ACCURACY)
    return total


def body(
    values,
    offsets,
    stiffness,
    leaf_basis,
    transfer,
    slab_transfer_matrices,
    leaf_coupling_matrices,
    leaf_admissible_mask,
    top_coupling,
    top_admissible,
):
    stacked = jnp.concatenate([offsets, stiffness[None], values], 0)
    padded = with_halo(stacked, (("blk", 1), ("along", 2)), 1, True)
    at_start = lax.axis_index("along") == 0
    at_finish = lax.axis_index("along") == lax.axis_size("along") - 1
    lower_rim = jnp.where(at_start, 0.0, padded[:, :, :1])
    upper_rim = jnp.where(at_finish, 0.0, padded[:, :, -1:])
    padded = jnp.concatenate([lower_rim, padded[:, :, 1:-1], upper_rim], 2)
    near = near_field(padded)
    coefs = jnp.einsum("slki,rsli->rslk", leaf_basis, values, precision=HIGHEST_ACCURACY)
    rimmed = with_halo(coefs, (("along", 2),), 1, False)
    far_leaf = jnp.zeros(coefs.shape, jnp.float32)
    sectors = lax.axis_size("blk")
    lower_window = rimmed
    upper_window = rimmed
    breadth = 1
    while breadth <= REACH:
        lower_came = passed_along(lower_window, "blk", breadth)
        upper_came = passed_along(upper_window, "blk", -breadth)
        lower_window = jnp.concatenate([lower_window, lower_came], 1)
        upper_window = jnp.concatenate([upper_window, upper_came], 1)
        breadth = 2 * breadth
    for distance in range(2, REACH + 1):
        far_leaf = add_sector(
            far_leaf,
            lower_window[:, distance : distance + 1],
            -distance,
            leaf_coupling_matrices,
            leaf_admissible_mask,
        )
        far_leaf = add_sector(
            far_leaf,
            upper_window[:, distance : distance + 1],
            distance,
            leaf_coupling_matrices,
            leaf_admissible_mask,
        )
    slab_coefficient_rows = jnp.einsum(
        "slqk,rslq->rsk", transfer, coefs, precision=HIGHEST_ACCURACY
    )
    shared_portion = jnp.einsum(
        "oxz,eox->eoz",
        slab_transfer_matrices[:, 0],
        slab_coefficient_rows,
        precision=HIGHEST_ACCURACY,
    )
    sector_coefs = lax.psum(shared_portion, "along")
    every_sector = lax.all_gather(sector_coefs, "blk", axis=1, tiled=True)
    sector = lax.axis_index("blk")
    others = jnp.arange(sectors, dtype=jnp.int32)
    apart = (others - sector) % sectors
    distant = jnp.logical_and(apart > REACH, apart < sectors - REACH).astype(jnp.float32)
    allowed = top_admissible[0].astype(jnp.float32) * distant
    sector_local_coefs = jnp.einsum(
        "stkq,rtq->rsk",
        top_coupling * allowed[None, :, None, None],
        every_sector,
        precision=HIGHEST_ACCURACY,
    )
    slab_local_coefs = jnp.einsum(
        "baz,lbz->lba", slab_transfer_matrices[:, 0], sector_local_coefs, precision=HIGHEST_ACCURACY
    )
    leaf_down = jnp.einsum("slqk,rsk->rslq", transfer, slab_local_coefs, precision=HIGHEST_ACCURACY)
    leaf_local = far_leaf + leaf_down
    return near + jnp.einsum("slki,rslk->rsli", leaf_basis, leaf_local, precision=HIGHEST_ACCURACY)


def solution(mesh):
    return jax.shard_map(
        body,
        mesh=mesh,
        in_specs=(
            P(None, "blk", "along", None),
            P(None, "blk", "along", None),
            P("blk", "along", None),
            P("blk", "along", None, None),
            P("blk", "along", None, None),
            P("blk", "along", None, None),
            P("blk", None, None, None),
            P("blk", None),
            P("blk", None, None, None),
            P("blk", None),
        ),
        out_specs=P(None, "blk", "along", None),
        check_vma=False,
    )
```

profile of v0, /device:TPU:0, one launch (start us, length us, event | category | flops | bytes accessed | tf_op | source)
XLA Modules:
  0.0 189.9 jit_solution(18029766824902312547)
XLA Ops:
  0.0 1.1 copy.17
  1.1 0.8 broadcast_in_dim.8
  1.9 0.9 copy.16
  2.8 0.7 pad_maximum_fusion.4
  3.5 5.5 %collective-permute-start.1 = (f32[7,1,24,256]{3,0,2,1:T(8,128)}, f32[7,1,24,256]{3,0,2,1:T(8,128)S(1)}, u32[]{:S(2)}, u32[]{:S(2)}) collective-permute-start(f32[7,1,24,256]{3,0,2,1:T(8,128)} %pad_maximum_fusion.4), channel_id=1, source_target_pairs={{2,0},{4,2},{6,4},{8,6},{10,8},{12,10},{14,12},{16,14},{18,16},{20... | collective-permute-start | bytes 516104 | tf_op jit(solution)/shard_map/ppermute | solution.py:22
  9.0 2.3 %fusion.200 = f32[24,3,64]{2,1,0:T(4,128)S(1)} fusion(f32[1,24,64,256]{3,2,1,0:T(8,128)S(1)} %copy-done, f32[3,24,256]{2,1,0:T(8,128)} %bitcast.397), kind=kOutput, calls=%fused_computation.200 | convolution fusion | flops 14155776 | bytes 1665024 | tf_op jit(solution)/shard_map/slki,rsli->rslk/dot_general | solution.py:95
  11.3 0.6 fusion.435
  11.9 1.3 collective-permute-start.5
  13.2 5.1 %collective-permute-start.4 = (f32[3,1,1,64]{3,0,2,1:T(4,128)}, f32[3,1,1,64]{3,0,2,1:T(4,128)}, u32[]{:S(2)}, u32[]{:S(2)}) collective-permute-start(f32[3,1,1,64]{3,0,2,1:T(4,128)} %get-tuple-element.78), channel_id=1, source_target_pairs={{0,1},{2,3},{4,5},{6,7},{8,9},{10,11},{12,13},{14,15},{16,17},{18,... | collective-permute-start | bytes 2312 | tf_op jit(solution)/shard_map/ppermute | solution.py:20
  18.3 0.6 slice_bitcast_fusion.48
  19.0 0.6 broadcast_multiply_fusion
  19.6 0.5 convolution_bitcast_fusion.3
  20.1 0.7 convolution_bitcast_fusion.2
  20.8 5.6 %psum.7 = f32[3,1,64]{2,0,1:T(4,128)} all-reduce(f32[3,1,64]{2,0,1:T(4,128)} %convolution_bitcast_fusion.2), channel_id=1, replica_groups=mesh['blk'=16,'along'=2] {'along'}, use_global_device_ids=true, to_apply=%region_0.1 | all-reduce | flops 192 | bytes 1536 | tf_op jit(solution)/shard_map/psum | solution.py:132
  26.5 19.9 %all_gather.3 = f32[3,16,64]{2,0,1:T(4,128)} all-gather(f32[3,1,64]{2,0,1:T(4,128)} %psum.7), channel_id=1, replica_groups=mesh['blk'=16,'along'=2] {'blk'}, dimensions={1}, use_global_device_ids=true | all-gather | bytes 13056 | tf_op jit(solution)/shard_map/all_gather | solution.py:133
  46.3 0.7 and_select_fusion
  47.0 1.3 convolution_bitcast_fusion
  48.3 0.9 convolution_bitcast_fusion.1
  49.3 0.7 pad_maximum_fusion.8
  50.0 0.4 collective-permute-start.6
  50.4 4.1 %collective-permute-start.8 = (f32[3,1,26,64]{3,0,2,1:T(4,128)S(1)}, f32[3,1,26,64]{3,0,2,1:T(4,128)S(1)}, u32[]{:S(2)}, u32[]{:S(2)}) collective-permute-start(f32[3,1,26,64]{3,0,2,1:T(4,128)S(1)} %pad_maximum_fusion.8), channel_id=1, source_target_pairs={{0,30},{2,0},{4,2},{6,4},{8,6},{10,8},{12,10},{14,12},{16,14},{18,... | collective-permute-start | bytes 59912 | tf_op jit(solution)/shard_map/ppermute | solution.py:31
  54.5 0.7 fusion.436
  55.2 1.1 collective-permute-done.6
  56.3 1.4 pad_maximum_fusion.5
  57.7 4.7 %collective-permute-start.9 = (f32[3,2,26,64]{3,0,2,1:T(4,128)S(1)}, f32[3,2,26,64]{3,0,2,1:T(4,128)S(1)}, u32[]{:S(2)}, u32[]{:S(2)}) collective-permute-start(f32[3,2,26,64]{3,0,2,1:T(4,128)S(1)} %get-tuple-element.77), channel_id=1, source_target_pairs={{0,28},{2,30},{4,0},{6,2},{8,4},{10,6},{12,8},{14,10},{16,12},{18,... | collective-permute-start | bytes 119816 | tf_op jit(solution)/shard_map/ppermute | solution.py:31
  62.4 0.7 fusion.437
  82.0 0.8 pad_maximum_fusion.1
  82.9 2.0 %collective-permute-start.10 = (f32[3,4,26,64]{3,0,2,1:T(4,128)S(1)}, f32[3,4,26,64]{3,0,2,1:T(4,128)S(1)}, u32[]{:S(2)}, u32[]{:S(2)}) collective-permute-start(f32[3,4,26,64]{3,0,2,1:T(4,128)S(1)} %get-tuple-element.74), channel_id=1, source_target_pairs={{0,8},{2,10},{4,12},{6,14},{8,16},{10,18},{12,20},{14,22},{16,24},... | collective-permute-start | bytes 239624 | tf_op jit(solution)/shard_map/ppermute | solution.py:31
  84.9 1.0 fusion.279
  85.9 0.2 fusion.281
  86.1 0.2 fusion.283
  86.4 0.2 fusion.285
  86.6 0.2 fusion.287
  86.8 0.2 fusion.289
  87.0 0.2 fusion.291
  87.3 0.2 fusion.293
  87.5 0.2 fusion.295
  87.7 0.2 fusion.297
  87.9 0.2 fusion.299
  88.1 0.2 fusion.301
  88.4 6.1 %collective-permute-done.11 = f32[3,4,26,64]{3,0,2,1:T(4,128)S(1)} collective-permute-done((f32[3,4,26,64]{3,0,2,1:T(4,128)S(1)}, f32[3,4,26,64]{3,0,2,1:T(4,128)S(1)}, u32[]{:S(2)}, u32[]{:S(2)}) %collective-permute-start.11) | collective-permute-done | bytes 79904 | tf_op jit(solution)/shard_map/ppermute | solution.py:31
  94.5 0.2 fusion.243
  94.7 0.2 fusion.245
  95.3 0.2 fusion.249
  95.5 0.2 fusion.251
  96.4 0.2 fusion.259
  96.6 0.2 fusion.261
  97.7 0.2 fusion.271
  97.9 0.2 fusion.273
  98.7 2.0 %convolution_add_fusion = f32[3,24,64]{2,0,1:T(4,128)S(1)} fusion(f32[3,64,1]{1,0,2:T(4,128)S(1)} %convolution_bitcast_fusion.1, f32[1,24,64,64]{3,2,1,0:T(8,128)S(1)} %copy-done.1, f32[3,24,64]{2,1,0:T(8,128)S(1)} %fusion.243, f32[3,24,64]{2,1,0:T(8,128)S(1)} %fusion.245, f32[3,24,64]{2,1,0:T(8,128)S(1)} %fusion.247, f32[3,24,64]{2,1,0:T(8,128)S(1)} %fusion.249, ...), kind=kOutput, calls=%fused_computation.213 | convolution fusion | flops 3677184 | bytes 965376 | tf_op jit(solution)/shard_map/slqk,rsk->rslq/dot_general | solution.py:148
  100.6 2.0 %collective-permute-start.2 = (f32[7,3,1,256]{3,0,2,1:T(8,128)S(1)}, f32[7,3,1,256]{3,0,2,1:T(8,128)S(1)}, u32[]{:S(2)}, u32[]{:S(2)}) collective-permute-start(f32[7,3,1,256]{3,0,2,1:T(8,128)S(1)} %get-tuple-element.31), channel_id=1, source_target_pairs={{0,1},{1,0},{2,3},{3,2},{4,5},{5,4},{6,7},{7,6},{8,9},{9,8},{10,11... | collective-permute-start | bytes 64520 | tf_op jit(solution)/shard_map/ppermute | solution.py:20
  102.9 1.6 collective-permute-done.2
  105.8 0.4 copy-done.10
  106.3 9.2 %fusion = f32[24,3,256]{2,1,0:T(4,128)S(1)} fusion(f32[24,256]{1,0:T(8,128)S(1)} %get-tuple-element.110, f32[24,256]{1,0:T(8,128)S(1)} %get-tuple-element.111, f32[24,256]{1,0:T(8,128)S(1)} %get-tuple-element.112, f32[24,256]{1,0:T(8,128)S(1)} %get-tuple-element.113, f32[24,256]{1,0:T(8,128)S(1)} %copy-done.11, f32[24,256]{1,0:T(8,128)S(1)} %copy-done.12, ...), kind=kOutput, calls=%fused_computation | convolution fusion | flops 73924608 | bytes 368640 | tf_op jit(solution)/shard_map/alij,ralj->rali/dot_general | solution.py:51
  115.5 9.1 %fusion.39 = f32[24,3,256]{2,1,0:T(4,128)S(1)} fusion(f32[24,256]{1,0:T(8,128)S(1)} %get-tuple-element.122, f32[24,256]{1,0:T(8,128)S(1)} %get-tuple-element.123, f32[24,256]{1,0:T(8,128)S(1)} %get-tuple-element.124, f32[24,256]{1,0:T(8,128)S(1)} %get-tuple-element.125, f32[24,256]{1,0:T(8,128)S(1)} %copy-done.11, f32[24,256]{1,0:T(8,128)S(1)} %copy-done.12, ...), kind=kOutput, calls=%fused_computation.39 | convolution fusion | flops 73924608 | bytes 368640 | tf_op jit(solution)/shard_map/alij,ralj->rali/dot_general | solution.py:51
  124.5 9.1 %fusion.26 = f32[24,3,256]{2,1,0:T(4,128)S(1)} fusion(f32[24,256]{1,0:T(8,128)S(1)} %get-tuple-element.114, f32[24,256]{1,0:T(8,128)S(1)} %get-tuple-element.115, f32[24,256]{1,0:T(8,128)S(1)} %get-tuple-element.118, f32[24,256]{1,0:T(8,128)S(1)} %get-tuple-element.119, f32[24,256]{1,0:T(8,128)S(1)} %copy-done.11, f32[24,256]{1,0:T(8,128)S(1)} %copy-done.12, ...), kind=kOutput, calls=%fused_computation.26 | convolution fusion | flops 73924608 | bytes 368640 | tf_op jit(solution)/shard_map/alij,ralj->rali/dot_general | solution.py:51
  133.6 9.1 %fusion.65 = f32[24,3,256]{2,1,0:T(4,128)S(1)} fusion(f32[24,256]{1,0:T(8,128)S(1)} %get-tuple-element.126, f32[24,256]{1,0:T(8,128)S(1)} %get-tuple-element.127, f32[24,256]{1,0:T(8,128)S(1)} %get-tuple-element.130, f32[24,256]{1,0:T(8,128)S(1)} %get-tuple-element.131, f32[24,256]{1,0:T(8,128)S(1)} %copy-done.11, f32[24,256]{1,0:T(8,128)S(1)} %copy-done.12, ...), kind=kOutput, calls=%fused_computation.65 | convolution fusion | flops 73924608 | bytes 368640 | tf_op jit(solution)/shard_map/alij,ralj->rali/dot_general | solution.py:51
  142.6 9.1 %fusion.78 = f32[24,3,256]{2,1,0:T(4,128)S(1)} fusion(f32[24,256]{1,0:T(8,128)S(1)} %get-tuple-element.134, f32[24,256]{1,0:T(8,128)S(1)} %get-tuple-element.135, f32[24,256]{1,0:T(8,128)S(1)} %get-tuple-element.136, f32[24,256]{1,0:T(8,128)S(1)} %get-tuple-element.137, f32[24,256]{1,0:T(8,128)S(1)} %copy-done.11, f32[24,256]{1,0:T(8,128)S(1)} %copy-done.12, ...), kind=kOutput, calls=%fused_computation.78 | convolution fusion | flops 73924608 | bytes 368640 | tf_op jit(solution)/shard_map/alij,ralj->rali/dot_general | solution.py:51
  151.7 9.1 %fusion.104 = f32[24,3,256]{2,1,0:T(4,128)S(1)} fusion(f32[24,256]{1,0:T(8,128)S(1)} %copy-done.11, f32[24,256]{1,0:T(8,128)S(1)} %get-tuple-element.133, f32[24,256]{1,0:T(8,128)S(1)} %copy-done.12, f32[24,256]{1,0:T(8,128)S(1)} %get-tuple-element.129, f32[24,256]{1,0:T(8,128)S(1)} %copy-done.10, f32[24,256]{1,0:T(8,128)S(1)} %get-tuple-element.121, ...), kind=kOutput, calls=%fused_computation.104 | convolution fusion | flops 73924608 | bytes 368640 | tf_op jit(solution)/shard_map/alij,ralj->rali/dot_general | solution.py:51
  160.8 9.1 %fusion.226 = f32[24,3,256]{2,1,0:T(4,128)S(1)} fusion(f32[24,3,256]{2,1,0:T(4,128)S(1)} %fusion.65, f32[24,3,256]{2,1,0:T(4,128)S(1)} %fusion.78, f32[24,3,256]{2,1,0:T(4,128)S(1)} %fusion.104, f32[24,256]{1,0:T(8,128)S(1)} %get-tuple-element.116, f32[24,256]{1,0:T(8,128)S(1)} %get-tuple-element.120, f32[24,256]{1,0:T(8,128)S(1)} %get-tuple-element.128, ...), kind=kOutput, calls=%fused_computation.210 | convolution fusion | flops 73979904 | bytes 663552 | tf_op jit(solution)/shard_map/alij,ralj->rali/dot_general | solution.py:51
  169.9 9.5 %fusion.217 = f32[24,3,256]{2,1,0:T(4,128)S(1)} fusion(f32[24,3,256]{2,1,0:T(4,128)S(1)} %fusion.26, f32[24,3,256]{2,1,0:T(4,128)S(1)} %fusion.39, f32[24,3,256]{2,1,0:T(4,128)S(1)} %fusion.226, f32[24,256]{1,0:T(8,128)S(1)} %copy-done.11, f32[24,256]{1,0:T(8,128)S(1)} %copy-done.12, f32[24,256]{1,0:T(8,128)S(1)} %copy-done.10, ...), kind=kOutput, calls=%fused_computation.207 | convolution fusion | flops 73979904 | bytes 491520 | tf_op jit(solution)/shard_map/alij,ralj->rali/dot_general | solution.py:51
  179.3 9.1 %fusion.232 = f32[24,3,256]{2,1,0:T(4,128)S(1)} fusion(f32[24,3,256]{2,1,0:T(4,128)S(1)} %fusion, f32[24,3,256]{2,1,0:T(4,128)S(1)} %fusion.217, f32[24,256]{1,0:T(8,128)S(1)} %get-tuple-element.138, f32[24,256]{1,0:T(8,128)S(1)} %get-tuple-element.139, f32[24,256]{1,0:T(8,128)S(1)} %get-tuple-element.140, f32[24,256]{1,0:T(8,128)S(1)} %get-tuple-element.141, ...), kind=kOutput, calls=%fused_computation.212 | convolution fusion | flops 73961472 | bytes 565248 | tf_op jit(solution)/shard_map/alij,ralj->rali/dot_general | solution.py:51
  188.4 0.9 fusion.205
  189.3 0.7 copy.20
  (82 shorter events, 3.9 us)
Async XLA Ops:
  0.0 9.0 %copy-start = (f32[1,24,64,256]{3,2,1,0:T(8,128)S(1)}, f32[1,24,64,256]{3,2,1,0:T(8,128)}, u32[]{:S(2)}) copy-start(f32[1,24,64,256]{3,2,1,0:T(8,128)} %param.13) | copy-start | bytes 4718596
  0.0 19.0 %copy-start.8 = (f32[1,24,256]{2,1,0:T(8,128)S(1)}, f32[1,24,256]{2,1,0:T(8,128)}, u32[]{:S(2)}) copy-start(f32[1,24,256]{2,1,0:T(8,128)} %param.12) | copy-start | bytes 73732
  0.0 18.3 %copy-start.6 = (f32[3,1,24,256]{3,2,1,0:T(8,128)S(1)}, f32[3,1,24,256]{3,2,1,0:T(8,128)}, u32[]{:S(2)}) copy-start(f32[3,1,24,256]{3,2,1,0:T(8,128)} %param.11) | copy-start | bytes 221188
  0.0 19.6 %copy-start.1 = (f32[1,24,64,64]{3,2,1,0:T(8,128)S(1)}, f32[1,24,64,64]{3,2,1,0:T(8,128)}, u32[]{:S(2)}) copy-start(f32[1,24,64,64]{3,2,1,0:T(8,128)} %param.14) | copy-start | bytes 1179652
  2.8 17.3 %copy-start.7 = (f32[1,1,64,64]{3,2,1,0:T(8,128)S(1)}, f32[1,1,64,64]{3,2,1,0:T(8,128)}, u32[]{:S(2)}) copy-start(f32[1,1,64,64]{3,2,1,0:T(8,128)} %param.15) | copy-start | bytes 49156
  2.8 44.2 %copy-start.3 = (f32[1,16,64,64]{3,2,1,0:T(8,128)S(1)}, f32[1,16,64,64]{3,2,1,0:T(8,128)}, u32[]{:S(2)}) copy-start(f32[1,16,64,64]{3,2,1,0:T(8,128)} %param.18) | copy-start | bytes 786436
  3.5 95.0 %collective-permute-start.1 = (f32[7,1,24,256]{3,0,2,1:T(8,128)}, f32[7,1,24,256]{3,0,2,1:T(8,128)S(1)}, u32[]{:S(2)}, u32[]{:S(2)}) collective-permute-start(f32[7,1,24,256]{3,0,2,1:T(8,128)} %pad_maximum_fusion.4), channel_id=1, source_target_pairs={{2,0},{4,2},{6,4},{8,6},{10,8},{12,10},{14,12},{16,14},{18,16},{20... | collective-permute-start | bytes 516104 | tf_op jit(solution)/shard_map/ppermute | solution.py:22
  9.0 89.5 %collective-permute-start = (f32[7,1,24,256]{3,0,2,1:T(8,128)}, f32[7,1,24,256]{3,0,2,1:T(8,128)S(1)}, u32[]{:S(2)}, u32[]{:S(2)}) collective-permute-start(f32[7,1,24,256]{3,0,2,1:T(8,128)} %pad_maximum_fusion.4), channel_id=1, source_target_pairs={{0,2},{2,4},{4,6},{6,8},{8,10},{10,12},{12,14},{14,16},{16,18},{18... | collective-permute-start | bytes 516104 | tf_op jit(solution)/shard_map/ppermute | solution.py:20
  9.0 45.4 %copy-start.4 = (s32[1,30]{1,0:T(1,128)S(1)}, s32[1,30]{1,0:T(1,128)}, u32[]{:S(2)}) copy-start(s32[1,30]{1,0:T(1,128)} %param.17) | copy-start | bytes 364
  11.9 37.3 %collective-permute-start.5 = (f32[3,1,1,64]{3,0,2,1:T(4,128)}, f32[3,1,1,64]{3,0,2,1:T(4,128)S(1)}, u32[]{:S(2)}, u32[]{:S(2)}) collective-permute-start(f32[3,1,1,64]{3,0,2,1:T(4,128)} %get-tuple-element.79), channel_id=1, source_target_pairs={{1,0},{3,2},{5,4},{7,6},{9,8},{11,10},{13,12},{15,14},{17,16},{19,... | collective-permute-start | bytes 2312 | tf_op jit(solution)/shard_map/ppermute | solution.py:22
  13.2 36.1 %collective-permute-start.4 = (f32[3,1,1,64]{3,0,2,1:T(4,128)}, f32[3,1,1,64]{3,0,2,1:T(4,128)}, u32[]{:S(2)}, u32[]{:S(2)}) collective-permute-start(f32[3,1,1,64]{3,0,2,1:T(4,128)} %get-tuple-element.78), channel_id=1, source_target_pairs={{0,1},{2,3},{4,5},{6,7},{8,9},{10,11},{12,13},{14,15},{16,17},{18,... | collective-permute-start | bytes 2312 | tf_op jit(solution)/shard_map/ppermute | solution.py:20
  50.0 6.3 %collective-permute-start.6 = (f32[3,1,26,64]{3,0,2,1:T(4,128)S(1)}, f32[3,1,26,64]{3,0,2,1:T(4,128)S(1)}, u32[]{:S(2)}, u32[]{:S(2)}) collective-permute-start(f32[3,1,26,64]{3,0,2,1:T(4,128)S(1)} %pad_maximum_fusion.8), channel_id=1, source_target_pairs={{0,2},{2,4},{4,6},{6,8},{8,10},{10,12},{12,14},{14,16},{16,18},{18... | collective-permute-start | bytes 59912 | tf_op jit(solution)/shard_map/ppermute | solution.py:31
  50.4 5.9 %collective-permute-start.8 = (f32[3,1,26,64]{3,0,2,1:T(4,128)S(1)}, f32[3,1,26,64]{3,0,2,1:T(4,128)S(1)}, u32[]{:S(2)}, u32[]{:S(2)}) collective-permute-start(f32[3,1,26,64]{3,0,2,1:T(4,128)S(1)} %pad_maximum_fusion.8), channel_id=1, source_target_pairs={{0,30},{2,0},{4,2},{6,4},{8,6},{10,8},{12,10},{14,12},{16,14},{18,... | collective-permute-start | bytes 59912 | tf_op jit(solution)/shard_map/ppermute | solution.py:31
  57.7 24.3 %collective-permute-start.7 = (f32[3,2,26,64]{3,0,2,1:T(4,128)}, f32[3,2,26,64]{3,0,2,1:T(4,128)S(1)}, u32[]{:S(2)}, u32[]{:S(2)}) collective-permute-start(f32[3,2,26,64]{3,0,2,1:T(4,128)} %get-tuple-element.76), channel_id=1, source_target_pairs={{0,4},{2,6},{4,8},{6,10},{8,12},{10,14},{12,16},{14,18},{16,20},{1... | collective-permute-start | bytes 119816 | tf_op jit(solution)/shard_map/ppermute | solution.py:31
  57.7 24.3 %collective-permute-start.9 = (f32[3,2,26,64]{3,0,2,1:T(4,128)S(1)}, f32[3,2,26,64]{3,0,2,1:T(4,128)S(1)}, u32[]{:S(2)}, u32[]{:S(2)}) collective-permute-start(f32[3,2,26,64]{3,0,2,1:T(4,128)S(1)} %get-tuple-element.77), channel_id=1, source_target_pairs={{0,28},{2,30},{4,0},{6,2},{8,4},{10,6},{12,8},{14,10},{16,12},{18,... | collective-permute-start | bytes 119816 | tf_op jit(solution)/shard_map/ppermute | solution.py:31
  63.1 22.8 %copy-start.2 = (f32[1,30,64,64]{3,2,1,0:T(8,128)S(1)}, f32[1,30,64,64]{3,2,1,0:T(8,128)}, u32[]{:S(2)}) copy-start(f32[1,30,64,64]{3,2,1,0:T(8,128)} %param.16) | copy-start | bytes 1474564
  82.8 11.7 %collective-permute-start.11 = (f32[3,4,26,64]{3,0,2,1:T(4,128)S(1)}, f32[3,4,26,64]{3,0,2,1:T(4,128)S(1)}, u32[]{:S(2)}, u32[]{:S(2)}) collective-permute-start(f32[3,4,26,64]{3,0,2,1:T(4,128)S(1)} %get-tuple-element.75), channel_id=1, source_target_pairs={{0,24},{2,26},{4,28},{6,30},{8,0},{10,2},{12,4},{14,6},{16,8},{18,... | collective-permute-start | bytes 239624 | tf_op jit(solution)/shard_map/ppermute | solution.py:31
  82.9 12.3 %collective-permute-start.10 = (f32[3,4,26,64]{3,0,2,1:T(4,128)S(1)}, f32[3,4,26,64]{3,0,2,1:T(4,128)S(1)}, u32[]{:S(2)}, u32[]{:S(2)}) collective-permute-start(f32[3,4,26,64]{3,0,2,1:T(4,128)S(1)} %get-tuple-element.74), channel_id=1, source_target_pairs={{0,8},{2,10},{4,12},{6,14},{8,16},{10,18},{12,20},{14,22},{16,24},... | collective-permute-start | bytes 239624 | tf_op jit(solution)/shard_map/ppermute | solution.py:31
  98.6 4.1 %collective-permute-start.3 = (f32[7,3,1,256]{3,0,2,1:T(8,128)S(1)}, f32[7,3,1,256]{3,0,2,1:T(8,128)S(1)}, u32[]{:S(2)}, u32[]{:S(2)}) collective-permute-start(f32[7,3,1,256]{3,0,2,1:T(8,128)S(1)} %get-tuple-element.32), channel_id=1, source_target_pairs={{1,0},{0,1},{3,2},{2,3},{5,4},{4,5},{7,6},{6,7},{9,8},{8,9},{11,10... | collective-permute-start | bytes 64520 | tf_op jit(solution)/shard_map/ppermute | solution.py:22
  100.6 3.9 %collective-permute-start.2 = (f32[7,3,1,256]{3,0,2,1:T(8,128)S(1)}, f32[7,3,1,256]{3,0,2,1:T(8,128)S(1)}, u32[]{:S(2)}, u32[]{:S(2)}) collective-permute-start(f32[7,3,1,256]{3,0,2,1:T(8,128)S(1)} %get-tuple-element.31), channel_id=1, source_target_pairs={{0,1},{1,0},{2,3},{3,2},{4,5},{5,4},{6,7},{7,6},{8,9},{9,8},{10,11... | collective-permute-start | bytes 64520 | tf_op jit(solution)/shard_map/ppermute | solution.py:20
  105.5 0.7 copy-start.10
  105.5 0.7 copy-start.11
  105.5 0.8 copy-start.12
  105.5 0.8 copy-start.13
  160.8 9.1 %copy-start.5 = (f32[3,1,24,256]{3,2,1,0:T(8,128)S(1)}, f32[3,1,24,256]{3,2,1,0:T(8,128)}, u32[]{:S(2)}) copy-start(f32[3,1,24,256]{3,2,1,0:T(8,128)} %param.10) | copy-start | bytes 221188
  160.8 9.1 %copy-start.9 = (f32[1,24,256]{2,1,0:T(8,128)S(1)}, f32[1,24,256]{2,1,0:T(8,128)}, u32[]{:S(2)}) copy-start(f32[1,24,256]{2,1,0:T(8,128)} %param.12) | copy-start | bytes 73732
where the time goes:
time: 191 us; the launch traced here: 190 us
  matrix products  97.9 us (51%)
  blocking collectives  25.5 us (13%)
  starting transfers between devices  25.3 us (13%)
  between operations  19.5 us (10%)
  waiting for transfers between devices  8.8 us (5%)
  local copies, waits for them, and re-layouts  6.93 us (4%)
  other arithmetic  6.05 us (3%)
    dot_general x9, matrix products, near_field(): jnp.einsum('alij,ralj->rali', kernel, source[4:], precision=HIGHEST_ACCUR...  82.1 us
    all_gather x1, blocking collectives, body(): every_sector = lax.all_gather(sector_coefs, 'blk', axis=1, tiled=True)  19.9 us
    ppermute x6, starting transfers between devices, passed_along(): return lax.ppermute(x, axis, [(i, (i + by) % count) for i in range(count)])  11.3 us
    ppermute x6, waiting for transfers between devices, passed_along(): return lax.ppermute(x, axis, [(i, (i + by) % count) for i in range(count)])  7.18 us
    dot_general x30, matrix products, add_sector(): jnp.einsum('skq,rslq->rslk', coupling, partner, precision=HIGHEST_ACCURACY)  7.17 us
    ppermute x3, starting transfers between devices, with_halo(): lax.ppermute(tail, axis, [(i, (i + 1) % count) for i in range(ends)])  7.16 us
    ppermute x3, starting transfers between devices, with_halo(): lax.ppermute(head, axis, [((i + 1) % count, i) for i in range(ends)])  6.83 us
    psum x1, blocking collectives, body(): sector_coefs = lax.psum(shared_portion, 'along')  5.63 us
  transfers between devices with their start and end apart: 12, of which 3 were waited for; matrix products, arithmetic and copies ran while one was open for 12% of the time, Pallas kernels for 0%

commit v1 on v0

--- a/solution.py
+++ b/solution.py
@@ -130,7 +130,12 @@
         precision=HIGHEST_ACCURACY,
     )
     sector_coefs = lax.psum(shared_portion, "along")
-    every_sector = lax.all_gather(sector_coefs, "blk", axis=1, tiled=True)
+    ring = [sector_coefs]
+    for hop in range(15):
+        ring.append(lax.ppermute(ring[-1], "blk", [(dev, (dev + 1) % 16) for dev in range(16)]))
+    every_sector = jnp.roll(
+        jnp.concatenate(ring[::-1], axis=1), (lax.axis_index("blk") + 1) * ring[0].shape[1], axis=1
+    )
     sector = lax.axis_index("blk")
     others = jnp.arange(sectors, dtype=jnp.int32)
     apart = (others - sector) % sectors

time: 191 us -> 240 us (1.26)
  waiting for transfers between devices: 8.8 us -> 58.5 us
  local copies, waits for them, and re-layouts: 6.93 us -> 27.4 us
  blocking collectives: 25.5 us -> 5.86 us
    ppermute x0 -> x15, waiting for transfers between devices: none -> 48.2 us  [body(): lax.ppermute(ring[-1], 'blk', [(dev, (dev + 1) % 16) for dev in range(16)])]
    all_gather x1 -> x0, blocking collectives: 19.9 us -> none  [body(): every_sector = lax.all_gather(sector_coefs, 'blk', axis=1, tiled=True)]
    unnamed x46 -> x93, local copies, waits for them, and re-layouts: 2.66 us -> 22.4 us
  transfers between devices with their start and end apart: 12 -> 27, of which waited for: 3 -> 19; matrix products, arithmetic and copies ran while one was open for 12% -> 16% of each run, Pallas kernels for 0% -> 0%
where the time goes in v1:
time: 240 us; the launch traced here: 238 us
  matrix products  96.4 us (40%)
  waiting for transfers between devices  58.5 us (24%)
  local copies, waits for them, and re-layouts  27.4 us (11%)
  starting transfers between devices  24.5 us (10%)
  between operations  19.3 us (8%)
  other arithmetic  6.65 us (3%)
  blocking collectives  5.86 us (2%)
    dot_general x9, matrix products, near_field(): jnp.einsum('alij,ralj->rali', kernel, source[4:], precision=HIGHEST_ACCUR...  82.1 us
    ppermute x15, waiting for transfers between devices, body(): lax.ppermute(ring[-1], 'blk', [(dev, (dev + 1) % 16) for dev in range(16)])  48.2 us
    unnamed x93, local copies, waits for them, and re-layouts  22.4 us
    ppermute x6, starting transfers between devices, passed_along(): return lax.ppermute(x, axis, [(i, (i + by) % count) for i in range(count)])  11.4 us
    ppermute x3, starting transfers between devices, with_halo(): lax.ppermute(head, axis, [((i + 1) % count, i) for i in range(ends)])  7.82 us
    ppermute x6, waiting for transfers between devices, passed_along(): return lax.ppermute(x, axis, [(i, (i + by) % count) for i in range(count)])  6.76 us
    dot_general x30, matrix products, add_sector(): jnp.einsum('skq,rslq->rslk', coupling, partner, precision=HIGHEST_ACCURACY)  6.41 us
    psum x1, blocking collectives, body(): sector_coefs = lax.psum(shared_portion, 'along')  5.86 us
  transfers between devices with their start and end apart: 27, of which 19 were waited for; matrix products, arithmetic and copies ran while one was open for 16% of the time, Pallas kernels for 0%

profile of v1, /device:TPU:0, one launch (start us, length us, event | category | flops | bytes accessed | tf_op | source)
XLA Modules:
  0.0 238.4 jit_solution(11362663102099953738)
XLA Ops:
  0.0 1.6 copy-done
  1.7 2.3 fusion.200
  4.6 5.9 %psum.7 = f32[3,1,64]{2,0,1:T(4,128)S(1)} all-reduce(f32[3,1,64]{2,0,1:T(4,128)S(1)} %convolution_bitcast_fusion.2), channel_id=1, replica_groups=mesh['blk'=16,'along'=2] {'along'}, use_global_device_ids=true, to_apply=%region_0.1 | all-reduce | flops 192 | bytes 1536 | tf_op jit(solution)/shard_map/psum | solution.py:132
  10.5 5.7 %collective-permute-done.12 = f32[3,1,64]{2,0,1:T(4,128)S(1)} collective-permute-done((f32[3,1,64]{2,0,1:T(4,128)S(1)}, f32[3,1,64]{2,0,1:T(4,128)S(1)}, u32[]{:S(2)}, u32[]{:S(2)}) %collective-permute-start.12) | collective-permute-done | bytes 800 | tf_op jit(solution)/shard_map/ppermute | solution.py:135
  16.3 5.5 %collective-permute-done.13 = f32[3,1,64]{2,0,1:T(4,128)S(1)} collective-permute-done((f32[3,1,64]{2,0,1:T(4,128)S(1)}, f32[3,1,64]{2,0,1:T(4,128)S(1)}, u32[]{:S(2)}, u32[]{:S(2)}) %collective-permute-start.13) | collective-permute-done | bytes 800 | tf_op jit(solution)/shard_map/ppermute | solution.py:135
  21.9 0.8 pad_maximum_fusion.4
  22.7 4.4 %collective-permute-start.1 = (f32[7,1,24,256]{3,0,2,1:T(8,128)}, f32[7,1,24,256]{3,0,2,1:T(8,128)S(1)}, u32[]{:S(2)}, u32[]{:S(2)}) collective-permute-start(f32[7,1,24,256]{3,0,2,1:T(8,128)} %pad_maximum_fusion.4), channel_id=1, source_target_pairs={{2,0},{4,2},{6,4},{8,6},{10,8},{12,10},{14,12},{16,14},{18,16},{20... | collective-permute-start | bytes 516104 | tf_op jit(solution)/shard_map/ppermute | solution.py:22
  28.2 1.3 collective-permute-start.5
  29.5 5.1 %collective-permute-start.4 = (f32[3,1,1,64]{3,0,2,1:T(4,128)}, f32[3,1,1,64]{3,0,2,1:T(4,128)}, u32[]{:S(2)}, u32[]{:S(2)}) collective-permute-start(f32[3,1,1,64]{3,0,2,1:T(4,128)} %get-tuple-element.78), channel_id=1, source_target_pairs={{0,1},{2,3},{4,5},{6,7},{8,9},{10,11},{12,13},{14,15},{16,17},{18,... | collective-permute-start | bytes 2312 | tf_op jit(solution)/shard_map/ppermute | solution.py:20
  35.7 1.4 slice_bitcast_fusion.48
  37.1 4.4 %collective-permute-done.16 = f32[3,1,64]{2,0,1:T(4,128)} collective-permute-done((f32[3,1,64]{2,0,1:T(4,128)S(1)}, f32[3,1,64]{2,0,1:T(4,128)}, u32[]{:S(2)}, u32[]{:S(2)}) %collective-permute-start.16) | collective-permute-done | bytes 800 | tf_op jit(solution)/shard_map/ppermute | solution.py:135
  41.5 1.3 broadcast_multiply_fusion
  42.9 4.7 %collective-permute-done.17 = f32[3,1,64]{2,0,1:T(4,128)} collective-permute-done((f32[3,1,64]{2,0,1:T(4,128)}, f32[3,1,64]{2,0,1:T(4,128)}, u32[]{:S(2)}, u32[]{:S(2)}) %collective-permute-start.17) | collective-permute-done | bytes 800 | tf_op jit(solution)/shard_map/ppermute | solution.py:135
  47.6 1.2 and_select_fusion
  48.7 4.7 %collective-permute-done.18 = f32[3,1,64]{2,0,1:T(4,128)S(1)} collective-permute-done((f32[3,1,64]{2,0,1:T(4,128)}, f32[3,1,64]{2,0,1:T(4,128)S(1)}, u32[]{:S(2)}, u32[]{:S(2)}) %collective-permute-start.18) | collective-permute-done | bytes 800 | tf_op jit(solution)/shard_map/ppermute | solution.py:135
  54.1 0.7 fusion.438
  54.8 5.1 %collective-permute-done.19 = f32[3,1,64]{2,0,1:T(4,128)} collective-permute-done((f32[3,1,64]{2,0,1:T(4,128)S(1)}, f32[3,1,64]{2,0,1:T(4,128)}, u32[]{:S(2)}, u32[]{:S(2)}) %collective-permute-start.19) | collective-permute-done | bytes 800 | tf_op jit(solution)/shard_map/ppermute | solution.py:135
  59.9 0.7 fusion.439
  60.6 5.3 %collective-permute-done.20 = f32[3,1,64]{2,0,1:T(4,128)} collective-permute-done((f32[3,1,64]{2,0,1:T(4,128)}, f32[3,1,64]{2,0,1:T(4,128)}, u32[]{:S(2)}, u32[]{:S(2)}) %collective-permute-start.20) | collective-permute-done | bytes 800 | tf_op jit(solution)/shard_map/ppermute | solution.py:135
  65.9 5.9 %collective-permute-done.21 = f32[3,1,64]{2,0,1:T(4,128)S(1)} collective-permute-done((f32[3,1,64]{2,0,1:T(4,128)}, f32[3,1,64]{2,0,1:T(4,128)S(1)}, u32[]{:S(2)}, u32[]{:S(2)}) %collective-permute-start.21) | collective-permute-done | bytes 800 | tf_op jit(solution)/shard_map/ppermute | solution.py:135
  76.2 1.4 collective-permute-done.22
  82.5 1.0 collective-permute-done.23
  89.1 0.8 collective-permute-done.24
  94.3 1.8 collective-permute-done.25
  96.1 0.7 pad_maximum_fusion.8
  96.8 4.5 %collective-permute-start.8 = (f32[3,1,26,64]{3,0,2,1:T(4,128)S(1)}, f32[3,1,26,64]{3,0,2,1:T(4,128)S(1)}, u32[]{:S(2)}, u32[]{:S(2)}) collective-permute-start(f32[3,1,26,64]{3,0,2,1:T(4,128)S(1)} %pad_maximum_fusion.8), channel_id=1, source_target_pairs={{0,30},{2,0},{4,2},{6,4},{8,6},{10,8},{12,10},{14,12},{16,14},{18,... | collective-permute-start | bytes 59912 | tf_op jit(solution)/shard_map/ppermute | solution.py:31
  102.0 0.7 constant_dynamic-update-slice_fusion.30
  102.7 0.7 constant_dynamic-update-slice_fusion.29
  104.0 0.7 constant_dynamic-update-slice_fusion.27
  105.4 0.7 constant_dynamic-update-slice_fusion.24
  106.1 0.7 constant_dynamic-update-slice_fusion.23
  108.1 0.7 constant_dynamic-update-slice_fusion.20
  109.5 0.7 constant_dynamic-update-slice_fusion.18
  110.2 0.7 constant_dynamic-update-slice_fusion.17
  110.8 0.7 constant_dynamic-update-slice_fusion.16
  111.5 0.7 constant_dynamic-update-slice_fusion.14
  112.2 0.7 constant_dynamic-update-slice_fusion.13
  113.6 0.7 constant_dynamic-update-slice_fusion.11
  114.9 0.7 constant_dynamic-update-slice_fusion.8
  115.6 0.7 constant_dynamic-update-slice_fusion.7
  117.7 0.7 constant_dynamic-update-slice_fusion.4
  119.7 0.7 constant_dynamic-update-slice_fusion.1
  120.4 0.7 constant_dynamic-update-slice_fusion
  121.1 1.2 convolution_bitcast_fusion
  122.3 0.7 pad_maximum_fusion.5
  123.1 4.7 %collective-permute-start.9 = (f32[3,2,26,64]{3,0,2,1:T(4,128)S(1)}, f32[3,2,26,64]{3,0,2,1:T(4,128)S(1)}, u32[]{:S(2)}, u32[]{:S(2)}) collective-permute-start(f32[3,2,26,64]{3,0,2,1:T(4,128)S(1)} %get-tuple-element.77), channel_id=1, source_target_pairs={{0,28},{2,30},{4,0},{6,2},{8,4},{10,6},{12,8},{14,10},{16,12},{18,... | collective-permute-start | bytes 119816 | tf_op jit(solution)/shard_map/ppermute | solution.py:31
  127.8 0.9 convolution_bitcast_fusion.1
  128.7 1.9 collective-permute-done.7
  130.7 0.8 pad_maximum_fusion.1
  131.9 1.6 collective-permute-start.10
  136.3 4.8 %collective-permute-done.11 = f32[3,4,26,64]{3,0,2,1:T(4,128)S(1)} collective-permute-done((f32[3,4,26,64]{3,0,2,1:T(4,128)S(1)}, f32[3,4,26,64]{3,0,2,1:T(4,128)S(1)}, u32[]{:S(2)}, u32[]{:S(2)}) %collective-permute-start.11) | collective-permute-done | bytes 79904 | tf_op jit(solution)/shard_map/ppermute | solution.py:31
  145.2 2.1 collective-permute-start.3
  147.3 1.9 convolution_add_fusion
  149.6 3.5 %collective-permute-done.2 = f32[7,3,1,256]{3,0,2,1:T(8,128)S(1)} collective-permute-done((f32[7,3,1,256]{3,0,2,1:T(8,128)S(1)}, f32[7,3,1,256]{3,0,2,1:T(8,128)S(1)}, u32[]{:S(2)}, u32[]{:S(2)}) %collective-permute-start.2) | collective-permute-done | bytes 21536 | tf_op jit(solution)/shard_map/ppermute | solution.py:20
  154.7 9.2 %fusion = f32[24,3,256]{2,1,0:T(4,128)S(1)} fusion(f32[24,256]{1,0:T(8,128)S(1)} %get-tuple-element.110, f32[24,256]{1,0:T(8,128)S(1)} %get-tuple-element.111, f32[24,256]{1,0:T(8,128)S(1)} %get-tuple-element.114, f32[24,256]{1,0:T(8,128)S(1)} %get-tuple-element.115, f32[24,256]{1,0:T(8,128)S(1)} %copy-done.12, f32[24,256]{1,0:T(8,128)S(1)} %copy-done.13, ...), kind=kOutput, calls=%fused_computation | convolution fusion | flops 73924608 | bytes 368640 | tf_op jit(solution)/shard_map/alij,ralj->rali/dot_general | solution.py:51
  164.0 9.1 %fusion.39 = f32[24,3,256]{2,1,0:T(4,128)S(1)} fusion(f32[24,256]{1,0:T(8,128)S(1)} %get-tuple-element.127, f32[24,256]{1,0:T(8,128)S(1)} %get-tuple-element.128, f32[24,256]{1,0:T(8,128)S(1)} %get-tuple-element.131, f32[24,256]{1,0:T(8,128)S(1)} %get-tuple-element.132, f32[24,256]{1,0:T(8,128)S(1)} %copy-done.12, f32[24,256]{1,0:T(8,128)S(1)} %copy-done.13, ...), kind=kOutput, calls=%fused_computation.39 | convolution fusion | flops 73924608 | bytes 368640 | tf_op jit(solution)/shard_map/alij,ralj->rali/dot_general | solution.py:51
  173.0 9.1 %fusion.26 = f32[24,3,256]{2,1,0:T(4,128)S(1)} fusion(f32[24,256]{1,0:T(8,128)S(1)} %get-tuple-element.118, f32[24,256]{1,0:T(8,128)S(1)} %get-tuple-element.119, f32[24,256]{1,0:T(8,128)S(1)} %get-tuple-element.122, f32[24,256]{1,0:T(8,128)S(1)} %get-tuple-element.123, f32[24,256]{1,0:T(8,128)S(1)} %copy-done.12, f32[24,256]{1,0:T(8,128)S(1)} %copy-done.13, ...), kind=kOutput, calls=%fused_computation.26 | convolution fusion | flops 73924608 | bytes 368640 | tf_op jit(solution)/shard_map/alij,ralj->rali/dot_general | solution.py:51
  182.1 9.1 %fusion.65 = f32[24,3,256]{2,1,0:T(4,128)S(1)} fusion(f32[24,256]{1,0:T(8,128)S(1)} %get-tuple-element.134, f32[24,256]{1,0:T(8,128)S(1)} %get-tuple-element.135, f32[24,256]{1,0:T(8,128)S(1)} %get-tuple-element.138, f32[24,256]{1,0:T(8,128)S(1)} %get-tuple-element.139, f32[24,256]{1,0:T(8,128)S(1)} %copy-done.12, f32[24,256]{1,0:T(8,128)S(1)} %copy-done.13, ...), kind=kOutput, calls=%fused_computation.65 | convolution fusion | flops 73924608 | bytes 368640 | tf_op jit(solution)/shard_map/alij,ralj->rali/dot_general | solution.py:51
  191.2 9.1 %fusion.78 = f32[24,3,256]{2,1,0:T(4,128)S(1)} fusion(f32[24,256]{1,0:T(8,128)S(1)} %get-tuple-element.133, f32[24,256]{1,0:T(8,128)S(1)} %get-tuple-element.129, f32[24,256]{1,0:T(8,128)S(1)} %get-tuple-element.117, f32[24,256]{1,0:T(8,128)S(1)} %get-tuple-element.113, f32[24,256]{1,0:T(8,128)S(1)} %copy-done.12, f32[24,256]{1,0:T(8,128)S(1)} %copy-done.13, ...), kind=kOutput, calls=%fused_computation.78 | convolution fusion | flops 73924608 | bytes 368640 | tf_op jit(solution)/shard_map/alij,ralj->rali/dot_general | solution.py:51
  200.2 9.1 %fusion.104 = f32[24,3,256]{2,1,0:T(4,128)S(1)} fusion(f32[24,256]{1,0:T(8,128)S(1)} %copy-done.12, f32[24,256]{1,0:T(8,128)S(1)} %get-tuple-element.141, f32[24,256]{1,0:T(8,128)S(1)} %copy-done.13, f32[24,256]{1,0:T(8,128)S(1)} %get-tuple-element.137, f32[24,256]{1,0:T(8,128)S(1)} %copy-done.11, f32[24,256]{1,0:T(8,128)S(1)} %get-tuple-element.125, ...), kind=kOutput, calls=%fused_computation.104 | convolution fusion | flops 73924608 | bytes 368640 | tf_op jit(solution)/shard_map/alij,ralj->rali/dot_general | solution.py:51
  209.3 9.1 %fusion.226 = f32[24,3,256]{2,1,0:T(4,128)S(1)} fusion(f32[24,3,256]{2,1,0:T(4,128)S(1)} %fusion.65, f32[24,3,256]{2,1,0:T(4,128)S(1)} %fusion.78, f32[24,3,256]{2,1,0:T(4,128)S(1)} %fusion.104, f32[24,256]{1,0:T(8,128)S(1)} %get-tuple-element.120, f32[24,256]{1,0:T(8,128)S(1)} %get-tuple-element.124, f32[24,256]{1,0:T(8,128)S(1)} %get-tuple-element.136, ...), kind=kOutput, calls=%fused_computation.210 | convolution fusion | flops 73979904 | bytes 663552 | tf_op jit(solution)/shard_map/alij,ralj->rali/dot_general | solution.py:51
  218.4 9.5 %fusion.217 = f32[24,3,256]{2,1,0:T(4,128)S(1)} fusion(f32[24,3,256]{2,1,0:T(4,128)S(1)} %fusion.26, f32[24,3,256]{2,1,0:T(4,128)S(1)} %fusion.39, f32[24,3,256]{2,1,0:T(4,128)S(1)} %fusion.226, f32[24,256]{1,0:T(8,128)S(1)} %copy-done.12, f32[24,256]{1,0:T(8,128)S(1)} %copy-done.13, f32[24,256]{1,0:T(8,128)S(1)} %copy-done.11, ...), kind=kOutput, calls=%fused_computation.207 | convolution fusion | flops 73979904 | bytes 491520 | tf_op jit(solution)/shard_map/alij,ralj->rali/dot_general | solution.py:51
  227.8 9.1 %fusion.232 = f32[24,3,256]{2,1,0:T(4,128)S(1)} fusion(f32[24,3,256]{2,1,0:T(4,128)S(1)} %fusion, f32[24,3,256]{2,1,0:T(4,128)S(1)} %fusion.217, f32[24,256]{1,0:T(8,128)S(1)} %get-tuple-element.112, f32[24,256]{1,0:T(8,128)S(1)} %get-tuple-element.116, f32[24,256]{1,0:T(8,128)S(1)} %get-tuple-element.126, f32[24,256]{1,0:T(8,128)S(1)} %get-tuple-element.130, ...), kind=kOutput, calls=%fused_computation.212 | convolution fusion | flops 73961472 | bytes 565248 | tf_op jit(solution)/shard_map/alij,ralj->rali/dot_general | solution.py:51
  236.9 0.9 fusion.205
  (159 shorter events, 22.0 us)
Async XLA Ops:
  0.0 1.7 copy-start
  0.0 16.2 %copy-start.5 = (f32[3,1,24,256]{3,2,1,0:T(8,128)S(1)}, f32[3,1,24,256]{3,2,1,0:T(8,128)}, u32[]{:S(2)}) copy-start(f32[3,1,24,256]{3,2,1,0:T(8,128)} %param.10) | copy-start | bytes 221188
  0.0 3.9 %copy-start.1 = (f32[1,24,64,64]{3,2,1,0:T(8,128)S(1)}, f32[1,24,64,64]{3,2,1,0:T(8,128)}, u32[]{:S(2)}) copy-start(f32[1,24,64,64]{3,2,1,0:T(8,128)} %param.14) | copy-start | bytes 1179652
  0.0 4.5 %copy-start.8 = (f32[1,1,64,64]{3,2,1,0:T(8,128)S(1)}, f32[1,1,64,64]{3,2,1,0:T(8,128)}, u32[]{:S(2)}) copy-start(f32[1,1,64,64]{3,2,1,0:T(8,128)} %param.15) | copy-start | bytes 49156
  0.0 16.2 %copy-start.9 = (f32[1,24,256]{2,1,0:T(8,128)S(1)}, f32[1,24,256]{2,1,0:T(8,128)}, u32[]{:S(2)}) copy-start(f32[1,24,256]{2,1,0:T(8,128)} %param.12) | copy-start | bytes 73732
  0.0 16.3 %copy-start.7 = (f32[3,1,24,256]{3,2,1,0:T(8,128)S(1)}, f32[3,1,24,256]{3,2,1,0:T(8,128)}, u32[]{:S(2)}) copy-start(f32[3,1,24,256]{3,2,1,0:T(8,128)} %param.11) | copy-start | bytes 221188
  1.7 52.4 %copy-start.4 = (s32[1,30]{1,0:T(1,128)S(1)}, s32[1,30]{1,0:T(1,128)}, u32[]{:S(2)}) copy-start(s32[1,30]{1,0:T(1,128)} %param.17) | copy-start | bytes 364
  3.9 117.2 %copy-start.3 = (f32[1,16,64,64]{3,2,1,0:T(8,128)S(1)}, f32[1,16,64,64]{3,2,1,0:T(8,128)}, u32[]{:S(2)}) copy-start(f32[1,16,64,64]{3,2,1,0:T(8,128)} %param.18) | copy-start | bytes 786436
  10.5 5.8 %copy-start.15 = (f32[3,1,64]{2,0,1:T(4,128)}, f32[3,1,64]{2,0,1:T(4,128)S(1)}, u32[]{:S(2)}) copy-start(f32[3,1,64]{2,0,1:T(4,128)S(1)} %psum.7) | copy-start | bytes 2308
  10.5 5.7 %collective-permute-start.12 = (f32[3,1,64]{2,0,1:T(4,128)S(1)}, f32[3,1,64]{2,0,1:T(4,128)S(1)}, u32[]{:S(2)}, u32[]{:S(2)}) collective-permute-start(f32[3,1,64]{2,0,1:T(4,128)S(1)} %psum.7), channel_id=1, source_target_pairs={{0,2},{2,4},{4,6},{6,8},{8,10},{10,12},{12,14},{14,16},{16,18},{18... | collective-permute-start | bytes 2312 | tf_op jit(solution)/shard_map/ppermute | solution.py:135
  16.2 5.7 %copy-start.16 = (f32[3,1,64]{2,0,1:T(4,128)}, f32[3,1,64]{2,0,1:T(4,128)S(1)}, u32[]{:S(2)}) copy-start(f32[3,1,64]{2,0,1:T(4,128)S(1)} %collective-permute-done.12) | copy-start | bytes 2308
  16.2 5.7 %collective-permute-start.13 = (f32[3,1,64]{2,0,1:T(4,128)S(1)}, f32[3,1,64]{2,0,1:T(4,128)S(1)}, u32[]{:S(2)}, u32[]{:S(2)}) collective-permute-start(f32[3,1,64]{2,0,1:T(4,128)S(1)} %collective-permute-done.12), channel_id=1, source_target_pairs={{0,2},{2,4},{4,6},{6,8},{8,10},{10,12},{12,14},{14,16},{16,18},{18... | collective-permute-start | bytes 2312 | tf_op jit(solution)/shard_map/ppermute | solution.py:135
  21.9 6.3 %copy-start.17 = (f32[3,1,64]{2,0,1:T(4,128)}, f32[3,1,64]{2,0,1:T(4,128)S(1)}, u32[]{:S(2)}) copy-start(f32[3,1,64]{2,0,1:T(4,128)S(1)} %collective-permute-done.13) | copy-start | bytes 2308
  21.9 5.7 %collective-permute-start.14 = (f32[3,1,64]{2,0,1:T(4,128)S(1)}, f32[3,1,64]{2,0,1:T(4,128)S(1)}, u32[]{:S(2)}, u32[]{:S(2)}) collective-permute-start(f32[3,1,64]{2,0,1:T(4,128)S(1)} %collective-permute-done.13), channel_id=1, source_target_pairs={{0,2},{2,4},{4,6},{6,8},{8,10},{10,12},{12,14},{14,16},{16,18},{18... | collective-permute-start | bytes 2312 | tf_op jit(solution)/shard_map/ppermute | solution.py:135
  22.7 122.5 %collective-permute-start.1 = (f32[7,1,24,256]{3,0,2,1:T(8,128)}, f32[7,1,24,256]{3,0,2,1:T(8,128)S(1)}, u32[]{:S(2)}, u32[]{:S(2)}) collective-permute-start(f32[7,1,24,256]{3,0,2,1:T(8,128)} %pad_maximum_fusion.4), channel_id=1, source_target_pairs={{2,0},{4,2},{6,4},{8,6},{10,8},{12,10},{14,12},{16,14},{18,16},{20... | collective-permute-start | bytes 516104 | tf_op jit(solution)/shard_map/ppermute | solution.py:22
  27.1 118.1 %collective-permute-start = (f32[7,1,24,256]{3,0,2,1:T(8,128)}, f32[7,1,24,256]{3,0,2,1:T(8,128)S(1)}, u32[]{:S(2)}, u32[]{:S(2)}) collective-permute-start(f32[7,1,24,256]{3,0,2,1:T(8,128)} %pad_maximum_fusion.4), channel_id=1, source_target_pairs={{0,2},{2,4},{4,6},{6,8},{8,10},{10,12},{12,14},{14,16},{16,18},{18... | collective-permute-start | bytes 516104 | tf_op jit(solution)/shard_map/ppermute | solution.py:20
  27.6 0.6 copy-start.18
  27.6 7.5 %collective-permute-start.15 = (f32[3,1,64]{2,0,1:T(4,128)S(1)}, f32[3,1,64]{2,0,1:T(4,128)S(1)}, u32[]{:S(2)}, u32[]{:S(2)}) collective-permute-start(f32[3,1,64]{2,0,1:T(4,128)S(1)} %collective-permute-done.14), channel_id=1, source_target_pairs={{0,2},{2,4},{4,6},{6,8},{8,10},{10,12},{12,14},{14,16},{16,18},{18... | collective-permute-start | bytes 2312 | tf_op jit(solution)/shard_map/ppermute | solution.py:135
  28.2 67.8 %collective-permute-start.5 = (f32[3,1,1,64]{3,0,2,1:T(4,128)}, f32[3,1,1,64]{3,0,2,1:T(4,128)S(1)}, u32[]{:S(2)}, u32[]{:S(2)}) collective-permute-start(f32[3,1,1,64]{3,0,2,1:T(4,128)} %get-tuple-element.79), channel_id=1, source_target_pairs={{1,0},{3,2},{5,4},{7,6},{9,8},{11,10},{13,12},{15,14},{17,16},{19,... | collective-permute-start | bytes 2312 | tf_op jit(solution)/shard_map/ppermute | solution.py:22
  29.5 66.6 %collective-permute-start.4 = (f32[3,1,1,64]{3,0,2,1:T(4,128)}, f32[3,1,1,64]{3,0,2,1:T(4,128)}, u32[]{:S(2)}, u32[]{:S(2)}) collective-permute-start(f32[3,1,1,64]{3,0,2,1:T(4,128)} %get-tuple-element.78), channel_id=1, source_target_pairs={{0,1},{2,3},{4,5},{6,7},{8,9},{10,11},{12,13},{14,15},{16,17},{18,... | collective-permute-start | bytes 2312 | tf_op jit(solution)/shard_map/ppermute | solution.py:20
  35.1 0.6 copy-start.19
  35.7 5.8 %collective-permute-start.16 = (f32[3,1,64]{2,0,1:T(4,128)S(1)}, f32[3,1,64]{2,0,1:T(4,128)}, u32[]{:S(2)}, u32[]{:S(2)}) collective-permute-start(f32[3,1,64]{2,0,1:T(4,128)S(1)} %collective-permute-done.15), channel_id=1, source_target_pairs={{0,2},{2,4},{4,6},{6,8},{8,10},{10,12},{12,14},{14,16},{16,18},{18... | collective-permute-start | bytes 2312 | tf_op jit(solution)/shard_map/ppermute | solution.py:135
  41.5 6.0 %collective-permute-start.17 = (f32[3,1,64]{2,0,1:T(4,128)}, f32[3,1,64]{2,0,1:T(4,128)}, u32[]{:S(2)}, u32[]{:S(2)}) collective-permute-start(f32[3,1,64]{2,0,1:T(4,128)} %collective-permute-done.16), channel_id=1, source_target_pairs={{0,2},{2,4},{4,6},{6,8},{8,10},{10,12},{12,14},{14,16},{16,18},{18... | collective-permute-start | bytes 2312 | tf_op jit(solution)/shard_map/ppermute | solution.py:135
  47.6 5.9 %collective-permute-start.18 = (f32[3,1,64]{2,0,1:T(4,128)}, f32[3,1,64]{2,0,1:T(4,128)S(1)}, u32[]{:S(2)}, u32[]{:S(2)}) collective-permute-start(f32[3,1,64]{2,0,1:T(4,128)} %collective-permute-done.17), channel_id=1, source_target_pairs={{0,2},{2,4},{4,6},{6,8},{8,10},{10,12},{12,14},{14,16},{16,18},{18... | collective-permute-start | bytes 2312 | tf_op jit(solution)/shard_map/ppermute | solution.py:135
  53.5 0.6 copy-start.20
  54.1 5.8 %collective-permute-start.19 = (f32[3,1,64]{2,0,1:T(4,128)S(1)}, f32[3,1,64]{2,0,1:T(4,128)}, u32[]{:S(2)}, u32[]{:S(2)}) collective-permute-start(f32[3,1,64]{2,0,1:T(4,128)S(1)} %collective-permute-done.18), channel_id=1, source_target_pairs={{0,2},{2,4},{4,6},{6,8},{8,10},{10,12},{12,14},{14,16},{16,18},{18... | collective-permute-start | bytes 2312 | tf_op jit(solution)/shard_map/ppermute | solution.py:135
  59.9 6.0 %collective-permute-start.20 = (f32[3,1,64]{2,0,1:T(4,128)}, f32[3,1,64]{2,0,1:T(4,128)}, u32[]{:S(2)}, u32[]{:S(2)}) collective-permute-start(f32[3,1,64]{2,0,1:T(4,128)} %collective-permute-done.19), channel_id=1, source_target_pairs={{0,2},{2,4},{4,6},{6,8},{8,10},{10,12},{12,14},{14,16},{16,18},{18... | collective-permute-start | bytes 2312 | tf_op jit(solution)/shard_map/ppermute | solution.py:135
  65.9 5.9 %collective-permute-start.21 = (f32[3,1,64]{2,0,1:T(4,128)}, f32[3,1,64]{2,0,1:T(4,128)S(1)}, u32[]{:S(2)}, u32[]{:S(2)}) collective-permute-start(f32[3,1,64]{2,0,1:T(4,128)} %collective-permute-done.20), channel_id=1, source_target_pairs={{0,2},{2,4},{4,6},{6,8},{8,10},{10,12},{12,14},{14,16},{16,18},{18... | collective-permute-start | bytes 2312 | tf_op jit(solution)/shard_map/ppermute | solution.py:135
  71.8 5.8 %collective-permute-start.22 = (f32[3,1,64]{2,0,1:T(4,128)S(1)}, f32[3,1,64]{2,0,1:T(4,128)}, u32[]{:S(2)}, u32[]{:S(2)}) collective-permute-start(f32[3,1,64]{2,0,1:T(4,128)S(1)} %collective-permute-done.21), channel_id=1, source_target_pairs={{0,2},{2,4},{4,6},{6,8},{8,10},{10,12},{12,14},{14,16},{16,18},{18... | collective-permute-start | bytes 2312 | tf_op jit(solution)/shard_map/ppermute | solution.py:135
  77.6 5.9 %collective-permute-start.23 = (f32[3,1,64]{2,0,1:T(4,128)}, f32[3,1,64]{2,0,1:T(4,128)S(1)}, u32[]{:S(2)}, u32[]{:S(2)}) collective-permute-start(f32[3,1,64]{2,0,1:T(4,128)} %collective-permute-done.22), channel_id=1, source_target_pairs={{0,2},{2,4},{4,6},{6,8},{8,10},{10,12},{12,14},{14,16},{16,18},{18... | collective-permute-start | bytes 2312 | tf_op jit(solution)/shard_map/ppermute | solution.py:135
  83.6 0.6 copy-start.21
  84.1 5.8 %collective-permute-start.24 = (f32[3,1,64]{2,0,1:T(4,128)S(1)}, f32[3,1,64]{2,0,1:T(4,128)}, u32[]{:S(2)}, u32[]{:S(2)}) collective-permute-start(f32[3,1,64]{2,0,1:T(4,128)S(1)} %collective-permute-done.23), channel_id=1, source_target_pairs={{0,2},{2,4},{4,6},{6,8},{8,10},{10,12},{12,14},{14,16},{16,18},{18... | collective-permute-start | bytes 2312 | tf_op jit(solution)/shard_map/ppermute | solution.py:135
  89.9 6.1 %collective-permute-start.25 = (f32[3,1,64]{2,0,1:T(4,128)}, f32[3,1,64]{2,0,1:T(4,128)}, u32[]{:S(2)}, u32[]{:S(2)}) collective-permute-start(f32[3,1,64]{2,0,1:T(4,128)} %collective-permute-done.24), channel_id=1, source_target_pairs={{0,2},{2,4},{4,6},{6,8},{8,10},{10,12},{12,14},{14,16},{16,18},{18... | collective-permute-start | bytes 2312 | tf_op jit(solution)/shard_map/ppermute | solution.py:135
  94.3 39.3 %copy-start.2 = (f32[1,30,64,64]{3,2,1,0:T(8,128)S(1)}, f32[1,30,64,64]{3,2,1,0:T(8,128)}, u32[]{:S(2)}) copy-start(f32[1,30,64,64]{3,2,1,0:T(8,128)} %param.16) | copy-start | bytes 1474564
  96.1 5.9 %collective-permute-start.26 = (f32[3,1,64]{2,0,1:T(4,128)}, f32[3,1,64]{2,0,1:T(4,128)S(1)}, u32[]{:S(2)}, u32[]{:S(2)}) collective-permute-start(f32[3,1,64]{2,0,1:T(4,128)} %collective-permute-done.25), channel_id=1, source_target_pairs={{0,2},{2,4},{4,6},{6,8},{8,10},{10,12},{12,14},{14,16},{16,18},{18... | collective-permute-start | bytes 2312 | tf_op jit(solution)/shard_map/ppermute | solution.py:135
  96.8 25.5 %collective-permute-start.6 = (f32[3,1,26,64]{3,0,2,1:T(4,128)S(1)}, f32[3,1,26,64]{3,0,2,1:T(4,128)S(1)}, u32[]{:S(2)}, u32[]{:S(2)}) collective-permute-start(f32[3,1,26,64]{3,0,2,1:T(4,128)S(1)} %pad_maximum_fusion.8), channel_id=1, source_target_pairs={{0,2},{2,4},{4,6},{6,8},{8,10},{10,12},{12,14},{14,16},{16,18},{18... | collective-permute-start | bytes 59912 | tf_op jit(solution)/shard_map/ppermute | solution.py:31
  96.8 25.5 %collective-permute-start.8 = (f32[3,1,26,64]{3,0,2,1:T(4,128)S(1)}, f32[3,1,26,64]{3,0,2,1:T(4,128)S(1)}, u32[]{:S(2)}, u32[]{:S(2)}) collective-permute-start(f32[3,1,26,64]{3,0,2,1:T(4,128)S(1)} %pad_maximum_fusion.8), channel_id=1, source_target_pairs={{0,30},{2,0},{4,2},{6,4},{8,6},{10,8},{12,10},{14,12},{16,14},{18,... | collective-permute-start | bytes 59912 | tf_op jit(solution)/shard_map/ppermute | solution.py:31
  123.0 7.6 %collective-permute-start.7 = (f32[3,2,26,64]{3,0,2,1:T(4,128)S(1)}, f32[3,2,26,64]{3,0,2,1:T(4,128)S(1)}, u32[]{:S(2)}, u32[]{:S(2)}) collective-permute-start(f32[3,2,26,64]{3,0,2,1:T(4,128)S(1)} %get-tuple-element.76), channel_id=1, source_target_pairs={{0,4},{2,6},{4,8},{6,10},{8,12},{10,14},{12,16},{14,18},{16,20},{1... | collective-permute-start | bytes 119816 | tf_op jit(solution)/shard_map/ppermute | solution.py:31
  123.1 7.6 %collective-permute-start.9 = (f32[3,2,26,64]{3,0,2,1:T(4,128)S(1)}, f32[3,2,26,64]{3,0,2,1:T(4,128)S(1)}, u32[]{:S(2)}, u32[]{:S(2)}) collective-permute-start(f32[3,2,26,64]{3,0,2,1:T(4,128)S(1)} %get-tuple-element.77), channel_id=1, source_target_pairs={{0,28},{2,30},{4,0},{6,2},{8,4},{10,6},{12,8},{14,10},{16,12},{18,... | collective-permute-start | bytes 119816 | tf_op jit(solution)/shard_map/ppermute | solution.py:31
  131.4 9.6 %collective-permute-start.11 = (f32[3,4,26,64]{3,0,2,1:T(4,128)S(1)}, f32[3,4,26,64]{3,0,2,1:T(4,128)S(1)}, u32[]{:S(2)}, u32[]{:S(2)}) collective-permute-start(f32[3,4,26,64]{3,0,2,1:T(4,128)S(1)} %get-tuple-element.75), channel_id=1, source_target_pairs={{0,24},{2,26},{4,28},{6,30},{8,0},{10,2},{12,4},{14,6},{16,8},{18,... | collective-permute-start | bytes 239624 | tf_op jit(solution)/shard_map/ppermute | solution.py:31
  131.9 9.9 %collective-permute-start.10 = (f32[3,4,26,64]{3,0,2,1:T(4,128)S(1)}, f32[3,4,26,64]{3,0,2,1:T(4,128)S(1)}, u32[]{:S(2)}, u32[]{:S(2)}) collective-permute-start(f32[3,4,26,64]{3,0,2,1:T(4,128)S(1)} %get-tuple-element.74), channel_id=1, source_target_pairs={{0,8},{2,10},{4,12},{6,14},{8,16},{10,18},{12,20},{14,22},{16,24},... | collective-permute-start | bytes 239624 | tf_op jit(solution)/shard_map/ppermute | solution.py:31
  145.2 4.1 %collective-permute-start.3 = (f32[7,3,1,256]{3,0,2,1:T(8,128)S(1)}, f32[7,3,1,256]{3,0,2,1:T(8,128)S(1)}, u32[]{:S(2)}, u32[]{:S(2)}) collective-permute-start(f32[7,3,1,256]{3,0,2,1:T(8,128)S(1)} %get-tuple-element.32), channel_id=1, source_target_pairs={{1,0},{0,1},{3,2},{2,3},{5,4},{4,5},{7,6},{6,7},{9,8},{8,9},{11,10... | collective-permute-start | bytes 64520 | tf_op jit(solution)/shard_map/ppermute | solution.py:22
  149.2 3.9 %collective-permute-start.2 = (f32[7,3,1,256]{3,0,2,1:T(8,128)S(1)}, f32[7,3,1,256]{3,0,2,1:T(8,128)S(1)}, u32[]{:S(2)}, u32[]{:S(2)}) collective-permute-start(f32[7,3,1,256]{3,0,2,1:T(8,128)S(1)} %get-tuple-element.31), channel_id=1, source_target_pairs={{0,1},{1,0},{2,3},{3,2},{4,5},{5,4},{6,7},{7,6},{8,9},{9,8},{10,11... | collective-permute-start | bytes 64520 | tf_op jit(solution)/shard_map/ppermute | solution.py:20
  154.0 0.7 copy-start.11
  154.0 0.7 copy-start.12
  154.0 0.8 copy-start.13
  154.0 0.8 copy-start.14
  209.3 9.1 %copy-start.6 = (f32[3,1,24,256]{3,2,1,0:T(8,128)S(1)}, f32[3,1,24,256]{3,2,1,0:T(8,128)}, u32[]{:S(2)}) copy-start(f32[3,1,24,256]{3,2,1,0:T(8,128)} %param.10) | copy-start | bytes 221188
  209.3 9.1 %copy-start.10 = (f32[1,24,256]{2,1,0:T(8,128)S(1)}, f32[1,24,256]{2,1,0:T(8,128)}, u32[]{:S(2)}) copy-start(f32[1,24,256]{2,1,0:T(8,128)} %param.12) | copy-start | bytes 73732
